TPU v7x, 16 devices: a 4x2x1 block of a 4x4x8 slice. The times are simulated.
16 devices in a mesh: dp: 2 (over y, z), tp: 8 (over x, core).
Axes of the slice: x: 4, y: 2, z: 1, core: 2. Of those that a mesh axis runs over, the one named last changes fastest.
The devices are a block of a 4x4x8 slice.
Arguments:
- x_norm: bfloat16 [1024, 1536], P(('dp', 'tp')), parts along dimension 0
- w_gate: bfloat16 [1536, 8960], P(None, 'tp')
- w_up: bfloat16 [1536, 8960], P(None, 'tp')
- w_down: bfloat16 [8960, 1536], P('tp')
- u_gate: bfloat16 [1024, 8960], P('dp', 'tp'), parts along dimension 0
- u_up: bfloat16 [1024, 8960], P('dp', 'tp'), parts along dimension 0
- grad_out: bfloat16 [1024, 1536], P(('dp', 'tp')), parts along dimension 0
Outputs:
- output 1: bfloat16 [1024, 1536], P(('dp', 'tp')), parts along dimension 0
- output 2: float32 [3072, 8960], P('dp', 'tp'), parts along dimension 0
- output 3: float32 [3072, 8960], P('dp', 'tp'), parts along dimension 0
- output 4: float32 [17920, 1536], P(('dp', 'tp')), parts along dimension 0
There are 2 independent parts. A program takes and returns all parts, laid end to end along the dimension named above; an argument that names none is the same for every part.
All inputs are finite; a program needn't handle non-finite values.
Results may differ from a plain program's by a relative error of at most 0.0130562.
Values are sent between devices in bfloat16 or wider.
A program may use at most 768 MiB of HBM per device.

v0:
```python
import jax
import jax.numpy as jnp
from jax import lax
from jax.sharding import PartitionSpec as P

CONTRACT_ROWS = (((0,), (0,)), ((), ()))
CONTRACT_COLS = (((1,), (1,)), ((), ()))


def solution(mesh):
    def local_backward(x_loc, wg_loc, wu_loc, wd_loc, ug_loc, uu_loc, dy_loc):
        x_all = lax.all_gather(x_loc, 'tp', axis=0, tiled=True)
        dy_all = lax.all_gather(dy_loc, 'tp', axis=0, tiled=True)
        gate_pre = ug_loc.astype(jnp.float32)
        up_pre = uu_loc.astype(jnp.float32)
        sig_gate = jax.nn.sigmoid(gate_pre)
        gate_act = gate_pre * sig_gate
        z_act = (gate_act * up_pre).astype(jnp.bfloat16)
        grad_down = lax.dot_general(z_act, dy_all, CONTRACT_ROWS, preferred_element_type=jnp.float32)
        grad_hid = lax.dot_general(dy_all, wd_loc, CONTRACT_COLS, preferred_element_type=jnp.float32)
        grad_up = (grad_hid * gate_act).astype(jnp.bfloat16)
        grad_gate = (grad_hid * up_pre * sig_gate * (1.0 + gate_pre * (1.0 - sig_gate))).astype(jnp.bfloat16)
        part_x = (lax.dot_general(grad_gate, wg_loc, CONTRACT_COLS, preferred_element_type=jnp.float32)
                  + lax.dot_general(grad_up, wu_loc, CONTRACT_COLS, preferred_element_type=jnp.float32))
        grad_x = lax.psum_scatter(part_x.astype(jnp.bfloat16), 'tp', scatter_dimension=0, tiled=True)
        grad_wg = lax.dot_general(x_all, grad_gate, CONTRACT_ROWS, preferred_element_type=jnp.float32)
        grad_wu = lax.dot_general(x_all, grad_up, CONTRACT_ROWS, preferred_element_type=jnp.float32)
        return grad_x, grad_wg, grad_wu, grad_down

    tok_spec = P(('dp', 'tp'), None)
    col_spec = P(None, 'tp')
    act_spec = P('dp', 'tp')
    return jax.shard_map(local_backward, mesh=mesh,
                         in_specs=(tok_spec, col_spec, col_spec, P('tp', None), act_spec, act_spec, tok_spec),
                         out_specs=(tok_spec, act_spec, act_spec, tok_spec),
                         check_vma=False)
```

profile of v0, /device:TPU:112, one launch (start us, length us, event | category | flops | bytes accessed | tf_op | source)
XLA Modules:
  0.0 93.3 jit_solution(18116449735634594721)
XLA Ops:
  7.2 0.0 copy-start
  7.2 0.1 all-gather.3.cloned.1.call-start
  7.3 0.7 all-gather.3.cloned.1.call-update
  8.0 0.1 all-gather.5.cloned.1.call-start
  8.1 0.7 all-gather.5.cloned.1.call-update
  8.8 0.1 reduce-scatter.2.cloned.1.call-start
  8.9 23.9 %all-gather.3.cloned.1.call-done = bf16[512,1536]{1,0:T(8,128)(2,1)} async-done(((bf16[64,1536]{1,0:T(8,128)(2,1)}), bf16[512,1536]{1,0:T(8,128)(2,1)}) %all-gather.3.cloned.1.call-update) | async-done | bytes 1572880 | tf_op jit(solution)/shard_map/all_gather | solution.py:13
  32.7 0.0 copy-done
  32.7 0.0 copy-start.1
  32.7 4.9 %fusion.3 = (bf16[512,1120]{0,1:T(8,128)(2,1)S(1)}, f32[512,1120]{0,1:T(8,128)S(1)}) fusion(bf16[512,1120]{0,1:T(8,128)(2,1)} %param.12, bf16[512,1120]{0,1:T(8,128)(2,1)} %param.11, bf16[512,1536]{1,0:T(8,128)(2,1)} %all-gather.3.cloned.1.call-done, bf16[1120,1536]{1,0:T(8,128)(2,1)S(1)} %copy-done), kind=kOutput, calls=%fused_computation.11 | convolution fusion | flops 1768488960 | bytes 10747904 | tf_op jit(solution)/shard_map/dot_general | solution.py:20
  37.6 0.0 copy-start.8
  37.6 0.0 copy-start.9
  37.7 0.0 copy-done.1
  37.7 0.0 copy-start.2
  37.7 0.0 copy-start.6
  37.7 2.2 %fusion.12 = f32[512,1536]{1,0:T(8,128)S(1)} fusion(bf16[512,1120]{0,1:T(8,128)(2,1)S(1)} %get-tuple-element.4, bf16[1536,1120]{0,1:T(8,128)(2,1)S(1)} %copy-done.1), kind=kOutput, calls=%fused_computation.20 | convolution fusion | flops 1761607680 | bytes 7733248 | tf_op jit(solution)/shard_map/dot_general | solution.py:23
  39.9 0.0 copy-done.8
  39.9 0.0 copy-done.9
  40.0 0.9 copy-done.2
  40.9 0.3 copy-done.6
  41.2 3.7 %fusion = bf16[512,1536]{1,0:T(8,128)(2,1)} fusion(f32[512,1536]{1,0:T(8,128)S(1)} %fusion.12, bf16[1536,1120]{0,1:T(8,128)(2,1)S(1)} %copy-done.2, f32[512,1120]{0,1:T(8,128)S(1)} %get-tuple-element.5, bf16[512,1120]{0,1:T(8,128)(2,1)S(1)} %copy-done.6), kind=kOutput, calls=%fused_computation.6 | convolution fusion | flops 1767194624 | bytes 11599872 | tf_op jit(solution)/shard_map/dot_general | solution.py:24
  44.9 0.1 reduce-scatter.2.cloned.1.call-update
  44.9 9.8 %all-gather.5.cloned.1.call-done = bf16[512,1536]{1,0:T(8,128)(2,1)} async-done(((bf16[64,1536]{1,0:T(8,128)(2,1)}), bf16[512,1536]{1,0:T(8,128)(2,1)}) %all-gather.5.cloned.1.call-update) | async-done | bytes 1572880 | tf_op jit(solution)/shard_map/all_gather | solution.py:12
  54.7 0.0 copy-start.3
  54.7 0.0 copy-start.5
  54.7 0.0 copy-start.7
  54.7 6.8 %convolution_bitcast_fusion.1 = f32[1536,1120]{0,1:T(8,128)} fusion(bf16[512,1120]{0,1:T(8,128)(2,1)} %copy-done.8, bf16[512,1536]{1,0:T(8,128)(2,1)} %all-gather.5.cloned.1.call-done), kind=kOutput, calls=%fused_computation.1 | convolution fusion | flops 1761607680 | bytes 9601024 | tf_op jit(solution)/shard_map/dot_general | solution.py:26
  61.5 0.0 copy-done.3
  61.5 0.0 copy-done.5
  61.5 0.0 copy-done.7
  61.5 0.0 copy-start.4
  61.5 0.0 copy-start.10
  61.5 5.0 %fusion.9 = f32[1120,1536]{1,0:T(8,128)} fusion(bf16[512,1536]{1,0:T(8,128)(2,1)S(1)} %copy-done.3, bf16[512,1120]{0,1:T(8,128)(2,1)S(1)} %copy-done.5, bf16[512,1120]{0,1:T(8,128)(2,1)S(1)} %copy-done.7), kind=kOutput, calls=%fused_computation.18 | convolution fusion | flops 1766195200 | bytes 10747904 | tf_op jit(solution)/shard_map/dot_general | solution.py:19
  66.5 0.0 copy-done.4
  66.5 0.0 copy-done.10
  66.5 4.9 %convolution_bitcast_fusion = f32[1536,1120]{0,1:T(8,128)} fusion(bf16[512,1536]{1,0:T(8,128)(2,1)S(1)} %copy-done.4, f32[512,1120]{0,1:T(8,128)S(1)} %copy-done.10, bf16[512,1120]{0,1:T(8,128)(2,1)S(1)} %copy-done.7), kind=kOutput, calls=%fused_computation | convolution fusion | flops 1765621760 | bytes 11894784 | tf_op jit(solution)/shard_map/dot_general | solution.py:27
  71.5 15.3 %reduce-scatter.2.cloned.1.call-done = bf16[64,1536]{1,0:T(8,128)(2,1)} async-done(((bf16[512,1536]{1,0:T(8,128)(2,1)}), bf16[64,1536]{1,0:T(8,128)(2,1)}) %reduce-scatter.2.cloned.1.call-update) | async-done | bytes 196624 | tf_op jit(solution)/shard_map/reduce_scatter | solution.py:25
Async XLA Ops:
  7.2 25.6 %copy-start = (bf16[1120,1536]{1,0:T(8,128)(2,1)S(1)}, bf16[1120,1536]{1,0:T(8,128)(2,1)}, u32[]{:S(2)}) copy-start(bf16[1120,1536]{1,0:T(8,128)(2,1)} %param.10) | copy-start | bytes 10321924
  7.2 25.5 %all-gather.3.cloned.1.call-start = ((), (), s32[]{:S(2)}) async-start(), calls=%async_computation.1 | async-start | bytes 1769472 | tf_op jit(solution)/shard_map/all_gather | solution.py:13
  8.0 46.7 %all-gather.5.cloned.1.call-start = ((), (), s32[]{:S(2)}) async-start(), calls=%async_computation.3 | async-start | bytes 1769472 | tf_op jit(solution)/shard_map/all_gather | solution.py:12
  8.8 77.9 %reduce-scatter.2.cloned.1.call-start = ((), (), s32[]{:S(2)}) async-start(), calls=%async_computation.2 | async-start | bytes 1769472 | tf_op jit(solution)/shard_map/reduce_scatter | solution.py:25
  32.7 4.9 %copy-start.1 = (bf16[1536,1120]{0,1:T(8,128)(2,1)S(1)}, bf16[1536,1120]{0,1:T(8,128)(2,1)}, u32[]{:S(2)}) copy-start(bf16[1536,1120]{0,1:T(8,128)(2,1)} %param.8) | copy-start | bytes 10321924
  37.6 2.3 %copy-start.8 = (bf16[512,1120]{0,1:T(8,128)(2,1)}, bf16[512,1120]{0,1:T(8,128)(2,1)S(1)}, u32[]{:S(2)}) copy-start(bf16[512,1120]{0,1:T(8,128)(2,1)S(1)} %get-tuple-element.4) | copy-start | bytes 3440644
  37.6 2.3 %copy-start.9 = (f32[512,1120]{0,1:T(8,128)}, f32[512,1120]{0,1:T(8,128)S(1)}, u32[]{:S(2)}) copy-start(f32[512,1120]{0,1:T(8,128)S(1)} %get-tuple-element.5) | copy-start | bytes 6881284
  37.7 3.2 %copy-start.2 = (bf16[1536,1120]{0,1:T(8,128)(2,1)S(1)}, bf16[1536,1120]{0,1:T(8,128)(2,1)}, u32[]{:S(2)}) copy-start(bf16[1536,1120]{0,1:T(8,128)(2,1)} %param.9) | copy-start | bytes 10321924
  37.7 3.5 %copy-start.6 = (bf16[512,1120]{0,1:T(8,128)(2,1)S(1)}, bf16[512,1120]{0,1:T(8,128)(2,1)}, u32[]{:S(2)}) copy-start(bf16[512,1120]{0,1:T(8,128)(2,1)} %param.11) | copy-start | bytes 3440644
  54.7 6.8 %copy-start.3 = (bf16[512,1536]{1,0:T(8,128)(2,1)S(1)}, bf16[512,1536]{1,0:T(8,128)(2,1)}, u32[]{:S(2)}) copy-start(bf16[512,1536]{1,0:T(8,128)(2,1)} %all-gather.3.cloned.1.call-done) | copy-start | bytes 4718596
  54.7 6.8 %copy-start.5 = (bf16[512,1120]{0,1:T(8,128)(2,1)S(1)}, bf16[512,1120]{0,1:T(8,128)(2,1)}, u32[]{:S(2)}) copy-start(bf16[512,1120]{0,1:T(8,128)(2,1)} %param.12) | copy-start | bytes 3440644
  54.7 6.8 %copy-start.7 = (bf16[512,1120]{0,1:T(8,128)(2,1)S(1)}, bf16[512,1120]{0,1:T(8,128)(2,1)}, u32[]{:S(2)}) copy-start(bf16[512,1120]{0,1:T(8,128)(2,1)} %param.11) | copy-start | bytes 3440644
  61.5 5.0 %copy-start.4 = (bf16[512,1536]{1,0:T(8,128)(2,1)S(1)}, bf16[512,1536]{1,0:T(8,128)(2,1)}, u32[]{:S(2)}) copy-start(bf16[512,1536]{1,0:T(8,128)(2,1)} %all-gather.5.cloned.1.call-done) | copy-start | bytes 4718596
  61.5 5.0 %copy-start.10 = (f32[512,1120]{0,1:T(8,128)S(1)}, f32[512,1120]{0,1:T(8,128)}, u32[]{:S(2)}) copy-start(f32[512,1120]{0,1:T(8,128)} %copy-done.9) | copy-start | bytes 6881284
Sparse Core Ops, SparseCore 0:
  9.6 23.0 all-gather.2
  34.3 20.3 all-gather.4
  57.6 29.0 reduce-scatter.1
where the time goes:
time: 93.4 us; the launch traced here: 93.3 us
  waiting for transfers between devices  50.4 us (54%)
  matrix products  27.5 us (29%)
  between operations  13.9 us (15%)
  local copies, waits for them, and re-layouts  1.3 us (1%)
    all_gather x1, waiting for transfers between devices, local_backward(): dy_all = lax.all_gather(dy_loc, 'tp', axis=0, tiled=True)  23.9 us
    reduce_scatter x1, waiting for transfers between devices, local_backward(): lax.psum_scatter(part_x.astype(jnp.bfloat16), 'tp', scatter_dimension=0,...  15.3 us
    all_gather x1, waiting for transfers between devices, local_backward(): x_all = lax.all_gather(x_loc, 'tp', axis=0, tiled=True)  9.81 us
    dot_general x1, matrix products, local_backward(): lax.dot_general(x_all, grad_gate, CONTRACT_ROWS, preferred_element_type=j...  6.75 us
    dot_general x1, matrix products, local_backward(): lax.dot_general(z_act, dy_all, CONTRACT_ROWS, preferred_element_type=jnp....  5.01 us
    dot_general x1, matrix products, local_backward(): lax.dot_general(x_all, grad_up, CONTRACT_ROWS, preferred_element_type=jnp...  4.93 us
    dot_general x1, matrix products, local_backward(): lax.dot_general(dy_all, wd_loc, CONTRACT_COLS, preferred_element_type=jnp...  4.9 us
    dot_general x1, matrix products, local_backward(): lax.dot_general(grad_up, wu_loc, CONTRACT_COLS, preferred_element_type=jn...  3.66 us
  transfers between devices with their start and end apart: 3, of which 3 were waited for; matrix products, arithmetic and copies ran while one was open for 29% of the time, Pallas kernels for 0%

commit v1 on v0

v1 whole, which is shorter than its diff:
```python
import functools

import jax
import jax.numpy as jnp
from jax import lax
from jax.experimental import pallas as pl
from jax.experimental.pallas import tpu as pltpu
from jax.sharding import PartitionSpec as P

MESH = pl.DeviceIdType.MESH
CONTRACT_ROWS = (((0,), (0,)), ((), ()))
CONTRACT_COLS = (((1,), (1,)), ((), ()))
HBM = pl.BlockSpec(memory_space=pltpu.HBM)
VMEM = pl.BlockSpec(memory_space=pltpu.VMEM)


def _tiles(total, size):
    return [(at, min(size, total - at)) for at in range(0, total, size)]


def exchange_kernel(chips, x_hbm, dy_hbm, wg_hbm, wu_hbm, wd_hbm, ug_hbm, uu_hbm,
                    dx_out, xb, dug, duu, dwd,
                    dyb, wg, wu, wd, ug, uu, act, slope, z, part, peer, summed, mid, fin,
                    load_sem, send_sem, recv_sem):
    own = dy_hbm.shape[0]
    half = own // 2
    rows = 2 * own
    hidden = dy_hbm.shape[1]
    width = ug_hbm.shape[0]
    me = lax.axis_index('tp')
    chip, core = me // 2, me % 2
    right = lax.rem(chip + 1, chips) * 2 + core
    left = lax.rem(chip + chips - 1, chips) * 2 + core
    partner = chip * 2 + 1 - core
    mine = pl.multiple_of(core * own, own)
    other = pl.multiple_of((1 - core) * own, own)

    loads = {}

    def load(name, src, dst):
        copy = pltpu.make_async_copy(src, dst, load_sem.at[len(loads)])
        copy.start()
        loads[name] = copy

    load('dy', dy_hbm, dyb.at[pl.ds(mine, own)])
    load('x', x_hbm, xb.at[pl.ds(mine, own)])
    for slot, ahead in enumerate((0, 1, chips - 1, 2)):
        at = pl.multiple_of(lax.rem(chip + ahead, chips) * rows, rows)
        load(f'ug{slot}', ug_hbm.at[:, pl.ds(at, rows)], ug.at[:, pl.ds(slot * rows, rows)])
        load(f'uu{slot}', uu_hbm.at[:, pl.ds(at, rows)], uu.at[:, pl.ds(slot * rows, rows)])
    load('wd', wd_hbm, wd)
    load('wg', wg_hbm, wg)
    load('wu', wu_hbm, wu)

    barrier = pltpu.get_barrier_semaphore()
    for device in (left, right, partner):
        pl.semaphore_signal(barrier, inc=1, device_id={'tp': device}, device_id_type=MESH)
    pl.semaphore_wait(barrier, 3)

    copies = []

    def remote(src, dst, device):
        at = len(copies)
        copy = pltpu.make_async_remote_copy(
            src_ref=src, dst_ref=dst, send_sem=send_sem.at[at], recv_sem=recv_sem.at[at],
            device_id={'tp': device}, device_id_type=MESH)
        copies.append(copy)
        copy.start()
        return copy

    def span(buf, slot, which):
        return buf.at[pl.ds(pl.multiple_of(slot * rows + mine + which * half, half), half)]

    def send_own(buf):
        full = buf.at[pl.ds(mine, own)]
        got = {}
        got['2a'] = remote(span(buf, 0, 0), span(buf, 2, 0), right)
        got['1b'] = remote(span(buf, 0, 1), span(buf, 1, 1), left)
        got['2b'] = remote(span(buf, 0, 1), span(buf, 2, 1), right)
        got['1a'] = remote(span(buf, 0, 0), span(buf, 1, 0), left)
        got['0'] = remote(full, full, partner)
        return got

    def share(buf, got, slot, which):
        key = f'{slot}{"ab"[which]}'
        got[key].wait_recv()
        piece = span(buf, slot, which)
        if key == '2a':
            got['3a'] = remote(piece, span(buf, 3, 0), right)
        if key == '1b':
            got['3b'] = remote(piece, span(buf, 3, 1), left)
        got['p' + key] = remote(piece, piece, partner)

    def gate():
        for slot in range(4):
            loads[f'ug{slot}'].wait()
            loads[f'uu{slot}'].wait()

        def body(i, _):
            at = pl.ds(pl.multiple_of(i * 32, 32), 32)
            gate_pre = ug[at, :].astype(jnp.float32)
            up_pre = uu[at, :].astype(jnp.float32)
            sig = jax.nn.sigmoid(gate_pre)
            gate_act = gate_pre * sig
            act[at, :] = gate_act
            slope[at, :] = sig * (1.0 + gate_pre * (1.0 - sig))
            z[at, :] = (gate_act * up_pre).astype(jnp.bfloat16)
            return 0

        lax.fori_loop(0, width // 32, body, 0)

    def hidden_grad(slot, count):
        at = slice(slot * rows, (slot + count) * rows)
        dy = dyb[at, :]
        for m0, m in _tiles(width, width // 2):
            f = slice(m0, m0 + m)
            g = lax.dot_general(wd[f, :], dy, CONTRACT_COLS, preferred_element_type=jnp.float32)
            duu[f, at] = (g * act[f, at]).astype(jnp.bfloat16)
            dug[f, at] = (g * uu[f, at].astype(jnp.float32) * slope[f, at]).astype(jnp.bfloat16)

    def input_grad(slot, count):
        at = slice(slot * rows, (slot + count) * rows)
        for n0, n in _tiles(hidden, hidden // 2):
            cols = slice(n0, n0 + n)
            total = (lax.dot_general(dug[:, at], wg[:, cols], CONTRACT_ROWS, preferred_element_type=jnp.float32)
                     + lax.dot_general(duu[:, at], wu[:, cols], CONTRACT_ROWS, preferred_element_type=jnp.float32))
            part[at, cols] = total.astype(jnp.bfloat16)

    def swap(slot):
        return remote(part.at[pl.ds(pl.multiple_of(slot * rows + other, own), own)],
                      peer.at[pl.ds(slot * own, own)], partner)

    def pair_sum(slot):
        a = part[pl.ds(pl.multiple_of(slot * rows + mine, own), own), :].astype(jnp.float32)
        return a + peer[slot * own:(slot + 1) * own, :].astype(jnp.float32)

    loads['dy'].wait()
    dy_got = send_own(dyb)
    gate()
    dy_got['0'].wait_recv()
    loads['wd'].wait()
    hidden_grad(0, 1)
    share(dyb, dy_got, 2, 0)
    share(dyb, dy_got, 1, 1)
    loads['x'].wait()
    x_got = send_own(xb)
    loads['wg'].wait()
    loads['wu'].wait()
    input_grad(0, 1)
    share(dyb, dy_got, 2, 1)
    share(dyb, dy_got, 1, 0)
    swaps = {0: swap(0)}
    for key in ('p2a', 'p1b', 'p2b', 'p1a'):
        dy_got[key].wait_recv()
    hidden_grad(1, 2)
    share(dyb, dy_got, 3, 0)
    share(dyb, dy_got, 3, 1)
    share(xb, x_got, 2, 0)
    share(xb, x_got, 1, 1)
    input_grad(1, 2)
    swaps[1] = swap(1)
    swaps[2] = swap(2)
    dy_got['p3a'].wait_recv()
    dy_got['p3b'].wait_recv()
    hidden_grad(3, 1)
    input_grad(3, 1)
    swaps[3] = swap(3)
    share(xb, x_got, 2, 1)
    share(xb, x_got, 1, 0)

    for slot in (1, 2):
        swaps[slot].wait_recv()
        summed[slot * own:(slot + 1) * own, :] = pair_sum(slot).astype(jnp.bfloat16)
    swaps[3].wait_recv()
    summed[3 * own:4 * own, :] = pair_sum(3).astype(jnp.bfloat16)

    def block(buf, slot, which):
        return buf.at[pl.ds(slot * own + which * half, half)]

    far_a = remote(block(summed, 3, 0), block(mid, 0, 0), right)
    far_b = remote(block(summed, 3, 1), block(mid, 0, 1), left)
    near_rb = remote(block(summed, 1, 1), block(fin, 1, 1), right)
    near_la = remote(block(summed, 2, 0), block(fin, 0, 0), left)
    swaps[0].wait_recv()
    for m0, m in _tiles(width, width // 4):
        dwd[m0:m0 + m, :] = jnp.dot(z[m0:m0 + m, :], dyb[...], preferred_element_type=jnp.float32)
    far_a.wait_recv()
    total = summed[own:own + half, :].astype(jnp.float32) + mid[:half, :].astype(jnp.float32)
    summed[0:half, :] = total.astype(jnp.bfloat16)
    near_ra = remote(block(summed, 0, 0), block(fin, 1, 0), right)
    far_b.wait_recv()
    total = summed[2 * own + half:3 * own, :].astype(jnp.float32) + mid[half:, :].astype(jnp.float32)
    summed[half:own, :] = total.astype(jnp.bfloat16)
    near_lb = remote(block(summed, 0, 1), block(fin, 0, 1), left)
    share(xb, x_got, 3, 0)
    share(xb, x_got, 3, 1)
    for copy in (near_rb, near_la, near_ra, near_lb):
        copy.wait_recv()
    dx = pair_sum(0) + fin[:own, :].astype(jnp.float32) + fin[own:, :].astype(jnp.float32)
    dx_out[...] = dx.astype(jnp.bfloat16)
    x_got['0'].wait_recv()
    for key in ('p2a', 'p1b', 'p2b', 'p1a', 'p3a', 'p3b'):
        x_got[key].wait_recv()
    for copy in copies:
        copy.wait_send()


def weight_kernel(dx, xb, dug, duu, dwd, dx_out, dwg_out, dwu_out, dwd_out, tile, sem, out_sem):
    tile_rows = tile.shape[1]
    slots = tile.shape[0]
    down = pltpu.make_async_copy(dwd, dwd_out, sem.at[0])
    down.start()
    small = pltpu.make_async_copy(dx, dx_out, sem.at[1])
    small.start()
    flying = {}
    step = 0
    for m0, m in _tiles(dug.shape[0], tile_rows):
        for grad, out in ((dug, dwg_out), (duu, dwu_out)):
            slot = step % slots
            if slot in flying:
                flying[slot].wait()
            tile[slot] = jnp.dot(grad[m0:m0 + m, :], xb[...], preferred_element_type=jnp.float32)
            copy = pltpu.make_async_copy(tile.at[slot], out.at[pl.ds(m0, m)], out_sem.at[slot])
            copy.start()
            flying[slot] = copy
            step += 1
    for copy in flying.values():
        copy.wait()
    down.wait()
    small.wait()


def solution(mesh):
    chips = mesh.shape['tp'] // 2

    def local_backward(x_loc, wg_loc, wu_loc, wd_loc, ug_loc, uu_loc, dy_loc):
        own, hidden = dy_loc.shape
        tokens, width = ug_loc.shape
        bf16, f32 = jnp.bfloat16, jnp.float32
        n_copies = 2 * (5 + 2 + 6) + 4 + 6
        dx, x_all, dug, duu, dwd = pl.pallas_call(
            functools.partial(exchange_kernel, chips),
            out_shape=[pltpu.VMEM((own, hidden), bf16),
                       pltpu.VMEM((tokens, hidden), bf16),
                       pltpu.VMEM((width, tokens), bf16),
                       pltpu.VMEM((width, tokens), bf16),
                       pltpu.VMEM((width, hidden), f32)],
            in_specs=[HBM] * 7,
            out_specs=[VMEM] * 5,
            scratch_shapes=[
                pltpu.VMEM((tokens, hidden), bf16),
                pltpu.VMEM((width, hidden), bf16),
                pltpu.VMEM((width, hidden), bf16),
                pltpu.VMEM((width, hidden), bf16),
                pltpu.VMEM((width, tokens), bf16),
                pltpu.VMEM((width, tokens), bf16),
                pltpu.VMEM((width, tokens), f32),
                pltpu.VMEM((width, tokens), f32),
                pltpu.VMEM((width, tokens), bf16),
                pltpu.VMEM((tokens, hidden), bf16),
                pltpu.VMEM((4 * own, hidden), bf16),
                pltpu.VMEM((4 * own, hidden), bf16),
                pltpu.VMEM((own, hidden), bf16),
                pltpu.VMEM((2 * own, hidden), bf16),
                pltpu.SemaphoreType.DMA((13,)),
                pltpu.SemaphoreType.DMA((n_copies,)),
                pltpu.SemaphoreType.DMA((n_copies,)),
            ],
            compiler_params=pltpu.CompilerParams(
                collective_id=0, has_side_effects=True, vmem_limit_bytes=44 * 2**20),
            name='exchange',
        )(x_loc, dy_loc, wg_loc.T, wu_loc.T, wd_loc, ug_loc.T, uu_loc.T)
        dx, dwg, dwu, dwd = pl.pallas_call(
            weight_kernel,
            out_shape=[jax.ShapeDtypeStruct((own, hidden), bf16)]
            + [jax.ShapeDtypeStruct((width, hidden), f32)] * 3,
            in_specs=[VMEM] * 5,
            out_specs=[HBM] * 4,
            scratch_shapes=[
                pltpu.VMEM((4, width // 4, hidden), f32),
                pltpu.SemaphoreType.DMA((2,)),
                pltpu.SemaphoreType.DMA((4,)),
            ],
            compiler_params=pltpu.CompilerParams(vmem_limit_bytes=24 * 2**20),
            name='weights',
        )(dx, x_all, dug, duu, dwd)
        return dx, dwg.T, dwu.T, dwd

    tok_spec = P(('dp', 'tp'), None)
    col_spec = P(None, 'tp')
    act_spec = P('dp', 'tp')
    return jax.shard_map(local_backward, mesh=mesh,
                         in_specs=(tok_spec, col_spec, col_spec, P('tp', None), act_spec, act_spec, tok_spec),
                         out_specs=(tok_spec, act_spec, act_spec, tok_spec),
                         check_vma=False)
```

time: 93.4 us -> 38.7 us (0.41)
  the two profiles are of different devices: /device:TPU:112 before, /device:TPU:113 now
where the time goes in v1:
time: 38.7 us; the launch traced here: 38.6 us
  Pallas kernels  38 us (98%)
  between operations  0.64 us (2%)
    pallas_call x1, Pallas kernels, local_backward(): pl.pallas_call(functools.partial(exchange_kernel, chips), out_shape=[pltp...  30.7 us
    pallas_call x1, Pallas kernels, local_backward(): pl.pallas_call(weight_kernel, out_shape=[jax.ShapeDtypeStruct((own, hidde...  7.28 us

profile of v1, /device:TPU:113, one launch (start us, length us, event | category | flops | bytes accessed | tf_op | source)
XLA Modules:
  0.0 38.6 jit_solution(6000210708507377741)
XLA Ops:
  0.6 30.7 %exchange.1 = (bf16[64,1536]{1,0:T(8,128)(2,1)S(1)}, bf16[512,1536]{1,0:T(8,128)(2,1)S(1)}, bf16[1120,512]{1,0:T(8,128)(2,1)S(1)}, bf16[1120,512]{1,0:T(8,128)(2,1)S(1)}, f32[1120,1536]{1,0:T(8,128)S(1)}) custom-call(bf16[64,1536]{1,0:T(8,128)(2,1)} %x_hbm.1, bf16[64,1536]{1,0:T(8,128)(2,1)} %dy_hbm.1, bf16[1120,1536]{1,0:T(8,128)(2,1)} %bitcast.6, ...), custom_call_target="tpu_custom_call" | custom-call | tf_op jit(solution)/shard_map/exchange/pallas_call | solution.py:241
  31.4 7.3 %weights.1 = (bf16[64,1536]{1,0:T(8,128)(2,1)}, f32[1120,1536]{1,0:T(8,128)}, f32[1120,1536]{1,0:T(8,128)}, f32[1120,1536]{1,0:T(8,128)}) custom-call(bf16[64,1536]{1,0:T(8,128)(2,1)S(1)} %get-tuple-element.13.dx, bf16[512,1536]{1,0:T(8,128)(2,1)S(1)} %get-tuple-element.14.xb, bf16[1120,512]{1,0:T(8,128)(2,1)S(1)} %get-tuple-element.15.dug, ...), custom_call_target="tpu_custom_call" | custom-call | tf_op jit(solution)/shard_map/weights/pallas_call | solution.py:273

commit v2 on v1

--- a/solution.py
+++ b/solution.py
@@ -19,8 +19,8 @@
 
 
 def exchange_kernel(chips, x_hbm, dy_hbm, wg_hbm, wu_hbm, wd_hbm, ug_hbm, uu_hbm,
-                    dx_out, xb, dug, duu, dwd,
-                    dyb, wg, wu, wd, ug, uu, act, slope, z, part, peer, summed, mid, fin,
+                    keep, fin, xb, dug, duu, dwd,
+                    dyb, wg, wu, wd, ug, uu, act, slope, z, part, peer, far, mid, near,
                     load_sem, send_sem, recv_sem):
     own = dy_hbm.shape[0]
     half = own // 2
@@ -71,15 +71,15 @@
     def span(buf, slot, which):
         return buf.at[pl.ds(pl.multiple_of(slot * rows + mine + which * half, half), half)]
 
-    def send_own(buf):
+    def send_first(buf):
         full = buf.at[pl.ds(mine, own)]
-        got = {}
-        got['2a'] = remote(span(buf, 0, 0), span(buf, 2, 0), right)
-        got['1b'] = remote(span(buf, 0, 1), span(buf, 1, 1), left)
+        return {'2a': remote(span(buf, 0, 0), span(buf, 2, 0), right),
+                '1b': remote(span(buf, 0, 1), span(buf, 1, 1), left),
+                '0': remote(full, full, partner)}
+
+    def send_second(buf, got):
         got['2b'] = remote(span(buf, 0, 1), span(buf, 2, 1), right)
         got['1a'] = remote(span(buf, 0, 0), span(buf, 1, 0), left)
-        got['0'] = remote(full, full, partner)
-        return got
 
     def share(buf, got, slot, which):
         key = f'{slot}{"ab"[which]}'
@@ -91,11 +91,7 @@
             got['3b'] = remote(piece, span(buf, 3, 1), left)
         got['p' + key] = remote(piece, piece, partner)
 
-    def gate():
-        for slot in range(4):
-            loads[f'ug{slot}'].wait()
-            loads[f'uu{slot}'].wait()
-
+    def gate(first, last):
         def body(i, _):
             at = pl.ds(pl.multiple_of(i * 32, 32), 32)
             gate_pre = ug[at, :].astype(jnp.float32)
@@ -107,7 +103,7 @@
             z[at, :] = (gate_act * up_pre).astype(jnp.bfloat16)
             return 0
 
-        lax.fori_loop(0, width // 32, body, 0)
+        lax.fori_loop(first, last, body, 0)
 
     def hidden_grad(slot, count):
         at = slice(slot * rows, (slot + count) * rows)
@@ -134,84 +130,95 @@
         a = part[pl.ds(pl.multiple_of(slot * rows + mine, own), own), :].astype(jnp.float32)
         return a + peer[slot * own:(slot + 1) * own, :].astype(jnp.float32)
 
+    def down_grad(index):
+        m = width // 4
+        at = slice(index * m, (index + 1) * m)
+        dwd[at, :] = jnp.dot(z[at, :], dyb[...], preferred_element_type=jnp.float32)
+
     loads['dy'].wait()
-    dy_got = send_own(dyb)
-    gate()
+    dy_got = send_first(dyb)
+    for slot in range(4):
+        loads[f'ug{slot}'].wait()
+        loads[f'uu{slot}'].wait()
+    steps = width // 32
+    gate(0, steps // 2)
+    send_second(dyb, dy_got)
+    gate(steps // 2, steps)
     dy_got['0'].wait_recv()
     loads['wd'].wait()
     hidden_grad(0, 1)
     share(dyb, dy_got, 2, 0)
     share(dyb, dy_got, 1, 1)
-    loads['x'].wait()
-    x_got = send_own(xb)
     loads['wg'].wait()
     loads['wu'].wait()
     input_grad(0, 1)
+    swaps = {0: swap(0)}
     share(dyb, dy_got, 2, 1)
     share(dyb, dy_got, 1, 0)
-    swaps = {0: swap(0)}
+    loads['x'].wait()
+    x_got = send_first(xb)
     for key in ('p2a', 'p1b', 'p2b', 'p1a'):
         dy_got[key].wait_recv()
     hidden_grad(1, 2)
     share(dyb, dy_got, 3, 0)
     share(dyb, dy_got, 3, 1)
-    share(xb, x_got, 2, 0)
-    share(xb, x_got, 1, 1)
-    input_grad(1, 2)
+    send_second(xb, x_got)
+    input_grad(1, 1)
     swaps[1] = swap(1)
-    swaps[2] = swap(2)
     dy_got['p3a'].wait_recv()
     dy_got['p3b'].wait_recv()
     hidden_grad(3, 1)
+    share(xb, x_got, 2, 0)
+    share(xb, x_got, 1, 1)
     input_grad(3, 1)
     swaps[3] = swap(3)
+    input_grad(2, 1)
+    swaps[2] = swap(2)
+
+    def block(buf, index, which):
+        return buf.at[pl.ds(index * own + which * half, half)]
+
+    swaps[3].wait_recv()
+    far[...] = pair_sum(3).astype(jnp.bfloat16)
+    far_a = remote(block(far, 0, 0), block(mid, 0, 0), right)
+    far_b = remote(block(far, 0, 1), block(mid, 0, 1), left)
     share(xb, x_got, 2, 1)
     share(xb, x_got, 1, 0)
-
-    for slot in (1, 2):
-        swaps[slot].wait_recv()
-        summed[slot * own:(slot + 1) * own, :] = pair_sum(slot).astype(jnp.bfloat16)
-    swaps[3].wait_recv()
-    summed[3 * own:4 * own, :] = pair_sum(3).astype(jnp.bfloat16)
-
-    def block(buf, slot, which):
-        return buf.at[pl.ds(slot * own + which * half, half)]
-
-    far_a = remote(block(summed, 3, 0), block(mid, 0, 0), right)
-    far_b = remote(block(summed, 3, 1), block(mid, 0, 1), left)
-    near_rb = remote(block(summed, 1, 1), block(fin, 1, 1), right)
-    near_la = remote(block(summed, 2, 0), block(fin, 0, 0), left)
-    swaps[0].wait_recv()
-    for m0, m in _tiles(width, width // 4):
-        dwd[m0:m0 + m, :] = jnp.dot(z[m0:m0 + m, :], dyb[...], preferred_element_type=jnp.float32)
-    far_a.wait_recv()
-    total = summed[own:own + half, :].astype(jnp.float32) + mid[:half, :].astype(jnp.float32)
-    summed[0:half, :] = total.astype(jnp.bfloat16)
-    near_ra = remote(block(summed, 0, 0), block(fin, 1, 0), right)
-    far_b.wait_recv()
-    total = summed[2 * own + half:3 * own, :].astype(jnp.float32) + mid[half:, :].astype(jnp.float32)
-    summed[half:own, :] = total.astype(jnp.bfloat16)
-    near_lb = remote(block(summed, 0, 1), block(fin, 0, 1), left)
+    down_grad(0)
+    down_grad(1)
+    swaps[1].wait_recv()
+    swaps[2].wait_recv()
+    near_r, near_l = pair_sum(1), pair_sum(2)
+    near[half:own, :] = near_r[half:].astype(jnp.bfloat16)
+    near[own:own + half, :] = near_l[:half].astype(jnp.bfloat16)
+    last = [remote(block(near, 0, 1), block(fin, 1, 1), right),
+            remote(block(near, 1, 0), block(fin, 0, 0), left)]
+    down_grad(2)
+    down_grad(3)
     share(xb, x_got, 3, 0)
     share(xb, x_got, 3, 1)
-    for copy in (near_rb, near_la, near_ra, near_lb):
+    far_a.wait_recv()
+    near[:half, :] = (near_r[:half] + mid[:half, :].astype(jnp.float32)).astype(jnp.bfloat16)
+    last.append(remote(block(near, 0, 0), block(fin, 1, 0), right))
+    far_b.wait_recv()
+    near[own + half:, :] = (near_l[half:] + mid[half:, :].astype(jnp.float32)).astype(jnp.bfloat16)
+    last.append(remote(block(near, 1, 1), block(fin, 0, 1), left))
+    swaps[0].wait_recv()
+    keep[...] = pair_sum(0)
+    for key in ('0', 'p2a', 'p1b', 'p2b', 'p1a', 'p3a', 'p3b'):
+        x_got[key].wait_recv()
+    for copy in last:
         copy.wait_recv()
-    dx = pair_sum(0) + fin[:own, :].astype(jnp.float32) + fin[own:, :].astype(jnp.float32)
-    dx_out[...] = dx.astype(jnp.bfloat16)
-    x_got['0'].wait_recv()
-    for key in ('p2a', 'p1b', 'p2b', 'p1a', 'p3a', 'p3b'):
-        x_got[key].wait_recv()
     for copy in copies:
         copy.wait_send()
 
 
-def weight_kernel(dx, xb, dug, duu, dwd, dx_out, dwg_out, dwu_out, dwd_out, tile, sem, out_sem):
+def weight_kernel(keep, fin, xb, dug, duu, dwd, dx_out, dwg_out, dwu_out, dwd_out, dx, tile, sem, out_sem):
+    own = keep.shape[0]
     tile_rows = tile.shape[1]
     slots = tile.shape[0]
     down = pltpu.make_async_copy(dwd, dwd_out, sem.at[0])
     down.start()
-    small = pltpu.make_async_copy(dx, dx_out, sem.at[1])
-    small.start()
     flying = {}
     step = 0
     for m0, m in _tiles(dug.shape[0], tile_rows):
@@ -224,6 +231,11 @@
             copy.start()
             flying[slot] = copy
             step += 1
+            if step == 2:
+                total = keep[...] + fin[:own, :].astype(jnp.float32) + fin[own:, :].astype(jnp.float32)
+                dx[...] = total.astype(jnp.bfloat16)
+                small = pltpu.make_async_copy(dx, dx_out, sem.at[1])
+                small.start()
     for copy in flying.values():
         copy.wait()
     down.wait()
@@ -238,15 +250,16 @@
         tokens, width = ug_loc.shape
         bf16, f32 = jnp.bfloat16, jnp.float32
         n_copies = 2 * (5 + 2 + 6) + 4 + 6
-        dx, x_all, dug, duu, dwd = pl.pallas_call(
+        keep, fin, x_all, dug, duu, dwd = pl.pallas_call(
             functools.partial(exchange_kernel, chips),
-            out_shape=[pltpu.VMEM((own, hidden), bf16),
+            out_shape=[pltpu.VMEM((own, hidden), f32),
+                       pltpu.VMEM((2 * own, hidden), bf16),
                        pltpu.VMEM((tokens, hidden), bf16),
                        pltpu.VMEM((width, tokens), bf16),
                        pltpu.VMEM((width, tokens), bf16),
                        pltpu.VMEM((width, hidden), f32)],
             in_specs=[HBM] * 7,
-            out_specs=[VMEM] * 5,
+            out_specs=[VMEM] * 6,
             scratch_shapes=[
                 pltpu.VMEM((tokens, hidden), bf16),
                 pltpu.VMEM((width, hidden), bf16),
@@ -259,7 +272,7 @@
                 pltpu.VMEM((width, tokens), bf16),
                 pltpu.VMEM((tokens, hidden), bf16),
                 pltpu.VMEM((4 * own, hidden), bf16),
-                pltpu.VMEM((4 * own, hidden), bf16),
+                pltpu.VMEM((own, hidden), bf16),
                 pltpu.VMEM((own, hidden), bf16),
                 pltpu.VMEM((2 * own, hidden), bf16),
                 pltpu.SemaphoreType.DMA((13,)),
@@ -274,16 +287,17 @@
             weight_kernel,
             out_shape=[jax.ShapeDtypeStruct((own, hidden), bf16)]
             + [jax.ShapeDtypeStruct((width, hidden), f32)] * 3,
-            in_specs=[VMEM] * 5,
+            in_specs=[VMEM] * 6,
             out_specs=[HBM] * 4,
             scratch_shapes=[
+                pltpu.VMEM((own, hidden), bf16),
                 pltpu.VMEM((4, width // 4, hidden), f32),
                 pltpu.SemaphoreType.DMA((2,)),
                 pltpu.SemaphoreType.DMA((4,)),
             ],
             compiler_params=pltpu.CompilerParams(vmem_limit_bytes=24 * 2**20),
             name='weights',
-        )(dx, x_all, dug, duu, dwd)
+        )(keep, fin, x_all, dug, duu, dwd)
         return dx, dwg.T, dwu.T, dwd
 
     tok_spec = P(('dp', 'tp'), None)

time: 38.7 us -> 36.1 us (0.933); the launches traced: 38.6 us -> 35.5 us
  Pallas kernels: 38 us -> 34.9 us
    pallas_call x1, Pallas kernels: 30.7 us -> 27.7 us  [local_backward(): pl.pallas_call(functools.partial(exchange_kernel, chips), out_shape=[pltp...]
where the time goes in v2:
time: 36.1 us; the launch traced here: 35.5 us
  Pallas kernels  34.9 us (97%)
  between operations  0.64 us (2%)
    pallas_call x1, Pallas kernels, local_backward(): pl.pallas_call(functools.partial(exchange_kernel, chips), out_shape=[pltp...  27.7 us
    pallas_call x1, Pallas kernels, local_backward(): pl.pallas_call(weight_kernel, out_shape=[jax.ShapeDtypeStruct((own, hidde...  7.22 us

profile of v2, /device:TPU:113, one launch (start us, length us, event | category | flops | bytes accessed | tf_op | source)
XLA Modules:
  0.0 35.5 jit_solution(1124864724054174943)
XLA Ops:
  0.6 27.7 %exchange.1 = (f32[64,1536]{1,0:T(8,128)S(1)}, bf16[128,1536]{1,0:T(8,128)(2,1)S(1)}, bf16[512,1536]{1,0:T(8,128)(2,1)S(1)}, bf16[1120,512]{1,0:T(8,128)(2,1)S(1...) custom-call(bf16[64,1536]{1,0:T(8,128)(2,1)} %x_hbm.1, bf16[64,1536]{1,0:T(8,128)(2,1)} %dy_hbm.1, ...), custom_call_target="tpu_custom_call" | custom-call | tf_op jit(solution)/shard_map/exchange/pallas_call | solution.py:253
  28.3 7.2 %weights.1 = (bf16[64,1536]{1,0:T(8,128)(2,1)}, f32[1120,1536]{1,0:T(8,128)}, f32[1120,1536]{1,0:T(8,128)}, f32[1120,1536]{1,0:T(8,128)}) custom-call(f32[64,1536]{1,0:T(8,128)S(1)} %get-tuple-element.14.keep, bf16[128,1536]{1,0:T(8,128)(2,1)S(1)} %get-tuple-element.15.fin, bf16[512,1536]{1,0:T(8,128)(2,1)S(1)} %get-tuple-element.16.xb, ...), custom_call_target="tpu_custom_call" | custom-call | tf_op jit(solution)/shard_map/weights/pallas_call | solution.py:286
